TPU v7x, 128 devices: a whole 4x4x4 slice. The times are simulated.
128 devices in a mesh: freq: 8 (over x, z_hi), panel: 16 (over z_lo, y, core).
Axes of the slice: x: 4, y: 4, z: 4 (z_hi: 2, z_lo: 2; z = z_hi * 2 + z_lo), core: 2. Of those that a mesh axis runs over, the one named last changes fastest.
Arguments:
- traces: bfloat16 [640, 640, 1024], P('panel', 'freq'), may hold values from -6 to 6
- filters: float32 [16, 7, 64], replicated, may hold values from -0.25 to 0.25
Outputs:
- primaries: bfloat16 [640, 640, 1024], P('panel', 'freq')
All inputs are finite; a program needn't handle non-finite values.
Results may differ from a plain program's by a relative error of at most 0.0095.
Values may be sent and summed in bfloat16 or wider, within the bound.
No kernel may reach another device: no remote copies, remote signals or barrier semaphores. Data moves between devices by JAX's collectives and lax.ppermute only.
A program may use at most 128 MiB of HBM per device.

v0:
```python
import math
import jax
import jax.numpy as jnp
from jax import lax
from jax.sharding import PartitionSpec as P

NS = 640
NT = 1024
NF = 96
FLO = 8
TAPS = 64
SPAN = 7
RWIN = 40


def wave_table(freq_bins, sample_index):
    phases = freq_bins[:, None] * sample_index[None, :] % NT
    angles = phases.astype(jnp.float32) * jnp.float32(2.0 * math.pi / NT)
    return (jnp.cos(angles), jnp.sin(angles))


def complex_product(left_side, right_side):

    def factor_product(leading_factor, trailing_factor):
        return jnp.einsum(
            "gjo,god->gjd", leading_factor, trailing_factor, preferred_element_type=jnp.float32
        )

    part_real = factor_product(left_side[0], right_side[0]) - factor_product(
        left_side[1], right_side[1]
    )
    part_imag = factor_product(left_side[0], right_side[1]) + factor_product(
        left_side[1], right_side[0]
    )
    return jnp.stack([part_real, part_imag])


def response(filters, freq_bins):
    tap_index = jnp.arange(TAPS, dtype=jnp.int32)
    cosine_wave, sine_wave = wave_table(freq_bins, tap_index)
    filter_real = jnp.einsum("fk,wjk->fjw", cosine_wave, filters)
    filter_imag = -jnp.einsum("fk,wjk->fjw", sine_wave, filters)
    return (jnp.repeat(filter_real, RWIN, axis=2), jnp.repeat(filter_imag, RWIN, axis=2))


def apply_filter(extended, filter_real, filter_imag, source_count):
    sum_real = jnp.zeros(extended.shape[1:2] + (source_count,) + extended.shape[3:], jnp.float32)
    sum_imag = jnp.zeros_like(sum_real)
    for shifted in range(SPAN):
        part_real = extended[0, :, shifted : shifted + source_count, :]
        part_imag = extended[1, :, shifted : shifted + source_count, :]
        weight_real = filter_real[:, shifted][:, None, :]
        weight_imaginary = filter_imag[:, shifted][:, None, :]
        sum_real = sum_real + weight_real * part_real - weight_imaginary * part_imag
        sum_imag = sum_imag + weight_real * part_imag + weight_imaginary * part_real
    return jnp.stack([sum_real, sum_imag])


def per_device(traces, filters):
    shot_rows, receiver_cols, time_sample_count = traces.shape
    rim_width = SPAN // 2
    scale_sources = jnp.float32(math.sqrt(NS))
    freq_bins = FLO + jnp.arange(NF, dtype=jnp.int32)
    cosine_wave, sine_wave = wave_table(freq_bins, jnp.arange(NT, dtype=jnp.int32))
    forward = (jnp.concatenate([cosine_wave, -sine_wave], 0) / jnp.float32(math.sqrt(NT))).astype(
        jnp.bfloat16
    )
    reciprocal_value = jnp.concatenate([cosine_wave, -sine_wave], 0).astype(jnp.bfloat16)
    spectra = jnp.einsum("srt,ct->csr", traces, forward, preferred_element_type=jnp.float32)
    spectra = spectra.astype(jnp.bfloat16).reshape(2, NF, shot_rows, receiver_cols)
    columns = lax.all_to_all(spectra, "panel", split_axis=1, concat_axis=2, tiled=True)
    slice_count = columns.shape[1]
    first_slice = lax.axis_index("panel") * slice_count
    complete = lax.all_gather(columns, "freq", axis=3, tiled=True)
    order_one = (complex_product(complete, columns) / scale_sources).astype(jnp.bfloat16)
    order_two = complex_product(complete, order_one) / scale_sources
    prediction = (order_one.astype(jnp.float32) - order_two).astype(jnp.bfloat16)
    extended = jnp.pad(
        prediction.astype(jnp.float32), ((0, 0), (0, 0), (rim_width, rim_width), (0, 0))
    )
    own_bins = FLO + first_slice + jnp.arange(slice_count, dtype=jnp.int32)
    filter_real, filter_imag = response(filters, own_bins)
    receiver_start = lax.axis_index("freq") * receiver_cols
    filter_real = lax.dynamic_slice_in_dim(filter_real, receiver_start, receiver_cols, 2)
    filter_imag = lax.dynamic_slice_in_dim(filter_imag, receiver_start, receiver_cols, 2)
    matched = apply_filter(extended, filter_real, filter_imag, NS)
    returned = lax.all_to_all(
        matched.astype(jnp.bfloat16), "panel", split_axis=2, concat_axis=1, tiled=True
    )
    matched_rows = returned.reshape(2 * NF, shot_rows, receiver_cols)
    multiples = jnp.einsum(
        "csr,ct->srt", matched_rows, reciprocal_value, preferred_element_type=jnp.float32
    )
    multiples = multiples / jnp.float32(math.sqrt(NF))
    return (traces.astype(jnp.float32) - multiples).astype(jnp.bfloat16)


def solution(mesh):
    placed = (P("panel", "freq", None), P())
    return jax.shard_map(
        per_device, mesh=mesh, in_specs=placed, out_specs=P("panel", "freq", None), check_vma=False
    )
```

profile of v0, /device:TPU:1, one launch (start us, length us, event | category | flops | bytes accessed | tf_op | source)
XLA Modules:
  0.0 312.2 jit_solution(14349941599640643925)
XLA Ops:
  6.5 1.6 fusion.58
  9.1 4.8 %convolution_convert_fusion = bf16[192,40,80]{0,2,1:T(8,128)(2,1)S(1)} fusion(bf16[40,80,1024]{2,1,0:T(8,128)(2,1)} %param.2, f32[96,1024]{1,0:T(8,128)S(1)} %get-tuple-element.24, f32[96,1024]{1,0:T(8,128)S(1)} %get-tuple-element.23), kind=kOutput, calls=%fused_computation.35 | convolution fusion | flops 1259495424 | bytes 8568832 | tf_op jit(solution)/shard_map/srt,ct->csr/dot_general | solution.py:69
  14.7 3.3 %copy.54 = bf16[2,96,40,80]{3,2,0,1:T(8,128)(2,1)} copy(bf16[2,96,40,80]{1,0,3,2:T(2,128)(2,1)S(1)} %reshape.26) | data formatting | bytes 2457600 | tf_op jit(solution)/shard_map/reshape | solution.py:70
  18.1 32.3 %all_to_all.33 = bf16[2,96,40,80]{3,2,0,1:T(8,128)(2,1)S(1)} all-to-all(bf16[2,96,40,80]{3,2,0,1:T(8,128)(2,1)} %copy.54), channel_id=1, replica_groups=mesh['freq'=8,'panel'=16] {'panel'}, dimensions={1} | all-to-all | bytes 2457600 | tf_op jit(solution)/shard_map/all_to_all | solution.py:71
  50.4 1.7 copy.56
  52.2 4.5 %copy.57 = bf16[2,6,640,80]{2,0,1,3:T(2,128)(2,1)} copy(bf16[2,6,640,80]{3,2,1,0:T(8,128)(2,1)} %bitcast.140) | data formatting | bytes 2457600 | tf_op jit(solution)/shard_map/all_to_all | solution.py:71
  59.3 118.6 %all-gather.2.cloned.1.call-done = bf16[2,6,640,640]{2,0,1,3:T(2,128)(2,1)} async-done(((bf16[2,6,640,80]{2,0,1,3:T(2,128)(2,1)}), bf16[2,6,640,640]{2,0,1,3:T(2,128)(2,1)}) %all-gather.2.cloned.1.call-update) | async-done | bytes 9830416 | tf_op jit(solution)/shard_map/all_gather | solution.py:74
  177.9 20.6 %fusion.80 = (bf16[1,6,640,640]{2,0,1,3:T(2,128)(2,1)}, bf16[1,6,640,640]{2,0,1,3:T(2,128)(2,1)}) fusion(bf16[2,6,640,640]{2,0,1,3:T(2,128)(2,1)} %all-gather.2.cloned.1.call-done), kind=kLoop, calls=%fused_computation.122 | loop fusion | bytes 19660800 | tf_op jit(solution)/shard_map/slice | solution.py:29
  198.5 19.7 %copy.91 = bf16[1,6,640,640]{3,2,1,0:T(8,128)(2,1)} copy(bf16[1,6,640,640]{2,0,1,3:T(2,128)(2,1)} %get-tuple-element.6) | data formatting | bytes 9830400
  218.3 19.8 %copy.90 = bf16[1,6,640,640]{3,2,1,0:T(8,128)(2,1)} copy(bf16[1,6,640,640]{2,0,1,3:T(2,128)(2,1)} %get-tuple-element.5) | data formatting | bytes 9830400
  238.0 4.2 %fusion.6 = f32[6,640,80]{1,2,0:T(8,128)S(1)} fusion(bf16[6,640,80]{2,1,0:T(8,128)(2,1)S(1)} %bitcast.133, bf16[1,6,640,640]{3,2,1,0:T(8,128)(2,1)} %copy.91), kind=kOutput, calls=%fused_computation.7 | convolution fusion | flops 393216000 | bytes 6758400 | tf_op jit(solution)/shard_map/gjo,god->gjd/dot_general | solution.py:25
  242.2 1.7 fusion.4
  244.6 1.7 fusion.23
  246.3 1.7 fusion.29
  248.2 1.7 fusion.2
  249.8 1.7 fusion
  251.5 1.7 fusion.35
  253.2 1.7 fusion.41
  255.2 5.4 %subtract_convert_fusion.1 = bf16[1,6,640,80]{2,3,1,0:T(8,128)(2,1)S(1)} fusion(f32[2,6,640,80]{2,3,1,0:T(8,128)S(1)} %fusion.44, f32[6,80]{1,0:T(8,128)S(1)} %bitcast.143, f32[6,80]{1,0:T(8,128)S(1)} %bitcast.145, f32[6,80]{1,0:T(8,128)S(1)} %bitcast.147, f32[6,80]{1,0:T(8,128)S(1)} %bitcast.149, f32[6,80]{1,0:T(8,128)S(1)} %bitcast.151, ...), kind=kLoop, calls=%fused_computation.47 | loop fusion | flops 8601600 | bytes 5586944 | tf_op jit(solution)/shard_map/convert
  260.6 5.3 %add_convert_fusion = bf16[1,6,640,80]{2,3,1,0:T(8,128)(2,1)S(1)} fusion(f32[2,6,640,80]{2,3,1,0:T(8,128)S(1)} %fusion.44, f32[6,80]{1,0:T(8,128)S(1)} %bitcast.144, f32[6,80]{1,0:T(8,128)S(1)} %bitcast.146, f32[6,80]{1,0:T(8,128)S(1)} %bitcast.148, f32[6,80]{1,0:T(8,128)S(1)} %bitcast.150, f32[6,80]{1,0:T(8,128)S(1)} %bitcast.152, ...), kind=kLoop, calls=%fused_computation.46 | loop fusion | flops 8601600 | bytes 5586944 | tf_op jit(solution)/shard_map/convert.1
  266.1 2.6 copy.67
  268.7 30.9 %all_to_all.34 = bf16[2,6,640,80]{3,0,1,2:T(2,128)(2,1)S(1)} all-to-all(bf16[2,6,640,80]{3,0,1,2:T(2,128)(2,1)S(1)} %copy.67), channel_id=1, replica_groups=mesh['freq'=8,'panel'=16] {'panel'}, dimensions={2} | all-to-all | bytes 2457600 | tf_op jit(solution)/shard_map/all_to_all | solution.py:87
  300.3 0.9 slice-done.1
  301.4 4.0 %subtract_convert_fusion = bf16[40,80,1024]{2,1,0:T(8,128)(2,1)} fusion(bf16[40,80,1024]{2,1,0:T(8,128)(2,1)S(1)} %bitcast.142, bf16[192,40,80]{2,1,0:T(8,128)(2,1)S(1)} %bitcast.138, f32[96,1024]{1,0:T(8,128)S(1)} %copy-done.7, f32[96,1024]{1,0:T(8,128)S(1)} %copy-done.5), kind=kOutput, calls=%fused_computation | convolution fusion | flops 1272184832 | bytes 15122432 | tf_op jit(solution)/shard_map/csr,ct->srt/dot_general | solution.py:91
  (57 shorter events, 6.6 us)
Async XLA Ops:
  6.5 50.2 %copy-start = (f32[16,7,64]{2,0,1:T(8,128)S(1)}, f32[16,7,64]{2,0,1:T(8,128)}, u32[]{:S(2)}) copy-start(f32[16,7,64]{2,0,1:T(8,128)} %param.3) | copy-start | bytes 86020
  6.5 171.3 %all-gather.2.cloned.1.call-start = ((), (), s32[]{:S(2)}) async-start(), calls=%async_computation.2 | async-start | bytes 11059200 | tf_op jit(solution)/shard_map/all_gather | solution.py:74
  8.2 0.8 copy-start.4
  8.2 0.9 copy-start.6
  238.0 4.2 %copy-start.2 = (bf16[1,6,640,640]{3,2,1,0:T(8,128)(2,1)S(1)}, bf16[1,6,640,640]{3,2,1,0:T(8,128)(2,1)}, u32[]{:S(2)}) copy-start(bf16[1,6,640,640]{3,2,1,0:T(8,128)(2,1)} %copy.91) | copy-start | bytes 14745604
  242.2 2.4 copy-start.3
  268.6 31.6 %slice-start = ((s8[6553600]{0:T(1024)(128)(4,1)}), s8[4194304]{0:T(1024)(128)(4,1)S(1)}, s32[]{:S(2)}) async-start(s8[6553600]{0:T(1024)(128)(4,1)} %bitcast.141), calls=%async_computation.3 | async-start | bytes 8388608
  299.5 1.7 slice-start.1
  299.9 1.4 copy-start.5
  299.9 1.5 copy-start.7
  301.4 4.0 %copy-start.1 = (f32[16,7,64]{2,0,1:T(8,128)S(1)}, f32[16,7,64]{2,0,1:T(8,128)}, u32[]{:S(2)}) copy-start(f32[16,7,64]{2,0,1:T(8,128)} %param.3) | copy-start | bytes 86020
Sparse Core Ops, SparseCore 0:
  56.8 120.9 all-gather.1
where the time goes:
time: 314 us; the launch traced here: 312 us
  waiting for transfers between devices  119 us (38%)
  local copies, waits for them, and re-layouts  78.6 us (25%)
  blocking collectives  63.2 us (20%)
  matrix products  25 us (8%)
  between operations  13.7 us (4%)
  other arithmetic  13.1 us (4%)
    all_gather x1, waiting for transfers between devices, per_device(): complete = lax.all_gather(columns, 'freq', axis=3, tiled=True)  119 us
    unnamed x36, local copies, waits for them, and re-layouts  42.4 us
    all_to_all x1, blocking collectives, per_device(): lax.all_to_all(spectra, 'panel', split_axis=1, concat_axis=2, tiled=True)  32.3 us
    all_to_all x1, blocking collectives, per_device(): lax.all_to_all(matched.astype(jnp.bfloat16), 'panel', split_axis=2, conca...  30.9 us
    slice x1, local copies, waits for them, and re-layouts, complex_product(): left_side[0]  20.6 us
    dot_general x8, matrix products, factor_product(): jnp.einsum('gjo,god->gjd', leading_factor, trailing_factor, preferred_ele...  15.8 us
    another operation x2, other arithmetic  10.7 us
    all_to_all x3, local copies, waits for them, and re-layouts, per_device(): lax.all_to_all(spectra, 'panel', split_axis=1, concat_axis=2, tiled=True)  6.6 us
  transfers between devices with their start and end apart: 1, of which 1 were waited for; matrix products, arithmetic and copies ran while one was open for 1% of the time, Pallas kernels for 0%

commit v1 on v0

--- a/solution.py
+++ b/solution.py
@@ -71,7 +71,9 @@
     columns = lax.all_to_all(spectra, "panel", split_axis=1, concat_axis=2, tiled=True)
     slice_count = columns.shape[1]
     first_slice = lax.axis_index("panel") * slice_count
-    complete = lax.all_gather(columns, "freq", axis=3, tiled=True)
+    complete = jnp.concatenate(
+        lax.all_to_all(jnp.stack([columns] * lax.axis_size("freq")), "freq", 0, 0), axis=3
+    )
     order_one = (complex_product(complete, columns) / scale_sources).astype(jnp.bfloat16)
     order_two = complex_product(complete, order_one) / scale_sources
     prediction = (order_one.astype(jnp.float32) - order_two).astype(jnp.bfloat16)

time: 314 us -> 271 us (0.86)
  local copies, waits for them, and re-layouts: 78.6 us -> 36.4 us
  between operations: 13.7 us -> 0.39 us
  waiting for transfers between devices: 119 us -> 132 us
  starting transfers between devices: 0.01 us -> 7.04 us
  matrix products: 25 us -> 19.6 us
    all_to_all x0 -> x1, waiting for transfers between devices: none -> 132 us  [per_device(): lax.all_to_all(jnp.stack([columns] * lax.axis_size('freq')), 'freq', 0, 0)]
    all_gather x1 -> x0, waiting for transfers between devices: 119 us -> none  [per_device(): complete = lax.all_gather(columns, 'freq', axis=3, tiled=True)]
    unnamed x36 -> x32, local copies, waits for them, and re-layouts: 42.4 us -> 2.41 us
    slice x1, local copies, waits for them, and re-layouts: 20.6 us -> 6.98 us  [complex_product(): left_side[1]]
    all_to_all x0 -> x1, local copies, waits for them, and re-layouts: none -> 8.72 us  [per_device(): lax.all_to_all(jnp.stack([columns] * lax.axis_size('freq')), 'freq', 0, 0)]
    another operation x0 -> x2, local copies, waits for them, and re-layouts: none -> 7.27 us  [per_device(): jnp.stack([columns] * lax.axis_size('freq'))]
    all_to_all x0 -> x1, starting transfers between devices: none -> 7.04 us  [per_device(): lax.all_to_all(jnp.stack([columns] * lax.axis_size('freq')), 'freq', 0, 0)]
    dot_general x8, matrix products: 15.8 us -> 10.4 us  [factor_product(): jnp.einsum('gjo,god->gjd', leading_factor, trailing_factor, preferred_ele...]
where the time goes in v1:
time: 271 us
  waiting for transfers between devices  132 us (49%)
  blocking collectives  62.4 us (23%)
  local copies, waits for them, and re-layouts  36.4 us (13%)
  matrix products  19.6 us (7%)
  other arithmetic  13.3 us (5%)
  starting transfers between devices  7.04 us (3%)
    all_to_all x1, waiting for transfers between devices, per_device(): lax.all_to_all(jnp.stack([columns] * lax.axis_size('freq')), 'freq', 0, 0)  132 us
    all_to_all x1, blocking collectives, per_device(): lax.all_to_all(spectra, 'panel', split_axis=1, concat_axis=2, tiled=True)  32.4 us
    all_to_all x1, blocking collectives, per_device(): lax.all_to_all(matched.astype(jnp.bfloat16), 'panel', split_axis=2, conca...  30 us
    another operation x2, other arithmetic  10.9 us
    dot_general x8, matrix products, factor_product(): jnp.einsum('gjo,god->gjd', leading_factor, trailing_factor, preferred_ele...  10.4 us
    all_to_all x1, local copies, waits for them, and re-layouts, per_device(): lax.all_to_all(jnp.stack([columns] * lax.axis_size('freq')), 'freq', 0, 0)  8.72 us
    another operation x2, local copies, waits for them, and re-layouts, per_device(): jnp.stack([columns] * lax.axis_size('freq'))  7.27 us
    all_to_all x1, starting transfers between devices, per_device(): lax.all_to_all(jnp.stack([columns] * lax.axis_size('freq')), 'freq', 0, 0)  7.04 us
  transfers between devices with their start and end apart: 1, of which 1 were waited for; matrix products, arithmetic and copies ran while one was open for 1% of the time, Pallas kernels for 0%

profile of v1, /device:TPU:1, one launch (start us, length us, event | category | flops | bytes accessed | tf_op | source)
XLA Modules:
  0.0 270.8 jit_solution(7768147361453043003)
XLA Ops:
  0.0 1.6 fusion.24
  2.5 4.8 %convolution_convert_fusion = bf16[192,40,80]{0,2,1:T(8,128)(2,1)S(1)} fusion(bf16[40,80,1024]{2,1,0:T(8,128)(2,1)} %param.2, f32[96,1024]{1,0:T(8,128)S(1)} %get-tuple-element.24, f32[96,1024]{1,0:T(8,128)S(1)} %get-tuple-element.23), kind=kOutput, calls=%fused_computation.20 | convolution fusion | flops 1259495424 | bytes 8568832 | tf_op jit(solution)/shard_map/srt,ct->csr/dot_general | solution.py:69
  8.1 3.3 %copy.54 = bf16[2,96,40,80]{3,2,0,1:T(8,128)(2,1)} copy(bf16[2,96,40,80]{1,0,3,2:T(2,128)(2,1)S(1)} %reshape.37) | data formatting | bytes 2457600 | tf_op jit(solution)/shard_map/reshape | solution.py:70
  11.5 32.4 %all_to_all.35 = bf16[2,96,40,80]{3,2,0,1:T(8,128)(2,1)S(1)} all-to-all(bf16[2,96,40,80]{3,2,0,1:T(8,128)(2,1)} %copy.54), channel_id=1, replica_groups=mesh['freq'=8,'panel'=16] {'panel'}, dimensions={1} | all-to-all | bytes 2457600 | tf_op jit(solution)/shard_map/all_to_all | solution.py:71
  43.8 1.7 copy.56
  45.6 2.7 %copy.57 = bf16[2,6,640,80]{2,3,1,0:T(8,128)(2,1)S(1)} copy(bf16[2,6,640,80]{3,2,1,0:T(8,128)(2,1)} %bitcast.128) | data formatting | bytes 2457600 | tf_op jit(solution)/shard_map/stack | solution.py:75
  48.3 4.6 %stack.38 = bf16[8,2,6,640,80]{3,4,2,1,0:T(8,128)(2,1)} broadcast(bf16[2,6,640,80]{2,3,1,0:T(8,128)(2,1)S(1)} %copy.57), dimensions={1,2,3,4} | broadcast | bytes 11059200 | tf_op jit(solution)/shard_map/stack | solution.py:75
  52.8 7.0 %all-to-all-start.1 = ((bf16[8,2,6,640,80]{3,4,2,1,0:T(8,128)(2,1)}), bf16[8,2,6,640,80]{3,4,2,1,0:T(8,128)(2,1)}, u32[]{:S(2)}, u32[]{:S(2)}) async-start(bf16[8,2,6,640,80]{3,4,2,1,0:T(8,128)(2,1)} %stack.38), calls=%async_computation.1 | async-start | bytes 19660800 | tf_op jit(solution)/shard_map/all_to_all | solution.py:75
  62.4 131.7 %all-to-all-done.1 = bf16[8,2,6,640,80]{3,4,2,1,0:T(8,128)(2,1)} async-done(((bf16[8,2,6,640,80]{3,4,2,1,0:T(8,128)(2,1)}), bf16[8,2,6,640,80]{3,4,2,1,0:T(8,128)(2,1)}, u32[]{:S(2)}, u32[]{:S(2)}) %all-to-all-start.1) | async-done | bytes 9830432 | tf_op jit(solution)/shard_map/all_to_all | solution.py:75
  194.2 8.7 %copy.122 = bf16[8,2,6,640,80]{3,4,0,2,1:T(8,128)(2,1)} copy(bf16[8,2,6,640,80]{3,4,2,1,0:T(8,128)(2,1)} %all-to-all-done.1) | data formatting | bytes 19660800 | tf_op jit(solution)/shard_map/all_to_all | solution.py:75
  202.9 7.0 %fusion.46 = (bf16[1,6,640,8,80]{2,4,3,1,0:T(8,128)(2,1)S(1)}, bf16[1,6,640,8,80]{2,4,3,1,0:T(8,128)(2,1)}) fusion(bf16[2,6,640,8,80]{2,4,3,1,0:T(8,128)(2,1)} %bitcast.119), kind=kLoop, calls=%fused_computation.109 | loop fusion | bytes 19660800 | tf_op jit(solution)/shard_map/slice | solution.py:30
  209.9 3.5 %fusion.50 = f32[6,640,80]{1,2,0:T(8,128)S(1)} fusion(bf16[6,640,640]{1,2,0:T(8,128)(2,1)} %bitcast.115, bf16[6,640,80]{2,1,0:T(8,128)(2,1)S(1)} %bitcast.121), kind=kOutput, calls=%fused_computation.113 | convolution fusion | flops 393216000 | bytes 6758400 | tf_op jit(solution)/shard_map/gjo,god->gjd/dot_general | solution.py:25
  213.7 1.0 fusion.51
  214.7 1.0 fusion.4
  215.7 1.0 fusion.5
  217.0 1.0 fusion.11
  217.9 1.0 fusion.12
  218.9 1.0 fusion.6
  219.9 1.0 fusion.7
  221.2 5.6 %subtract_convert_fusion.1 = bf16[1,6,640,80]{2,3,1,0:T(8,128)(2,1)S(1)} fusion(f32[2,6,640,80]{2,3,1,0:T(8,128)S(1)} %fusion.8, f32[6,80]{1,0:T(8,128)S(1)} %bitcast.153, f32[6,80]{1,0:T(8,128)S(1)} %bitcast.155, f32[6,80]{1,0:T(8,128)S(1)} %bitcast.157, f32[6,80]{1,0:T(8,128)S(1)} %bitcast.131, f32[6,80]{1,0:T(8,128)S(1)} %bitcast.133, ...), kind=kLoop, calls=%fused_computation.32 | loop fusion | flops 8601600 | bytes 5586944 | tf_op jit(solution)/shard_map/convert
  226.8 5.3 %add_convert_fusion = bf16[1,6,640,80]{2,3,1,0:T(8,128)(2,1)S(1)} fusion(f32[2,6,640,80]{2,3,1,0:T(8,128)S(1)} %fusion.8, f32[6,80]{1,0:T(8,128)S(1)} %bitcast.154, f32[6,80]{1,0:T(8,128)S(1)} %bitcast.156, f32[6,80]{1,0:T(8,128)S(1)} %bitcast.158, f32[6,80]{1,0:T(8,128)S(1)} %bitcast.132, f32[6,80]{1,0:T(8,128)S(1)} %bitcast.134, f32[6,80]{1,0:T(8,128)S(1)} %bitcast.136, ...), kind=kLoop, calls=%fused_computation.31 | loop fusion | flops 8601600 | bytes 5586944 | tf_op jit(solution)/shard_map/convert.1
  232.3 2.6 copy.74
  234.9 30.0 %all_to_all.36 = bf16[2,6,640,80]{3,0,1,2:T(2,128)(2,1)S(1)} all-to-all(bf16[2,6,640,80]{3,0,1,2:T(2,128)(2,1)S(1)} %copy.74), channel_id=1, replica_groups=mesh['freq'=8,'panel'=16] {'panel'}, dimensions={2} | all-to-all | bytes 2457600 | tf_op jit(solution)/shard_map/all_to_all | solution.py:89
  266.8 4.0 %subtract_convert_fusion = bf16[40,80,1024]{2,1,0:T(8,128)(2,1)} fusion(bf16[40,80,1024]{2,1,0:T(8,128)(2,1)S(1)} %bitcast.130, bf16[192,40,80]{2,1,0:T(8,128)(2,1)S(1)} %bitcast.126, f32[96,1024]{1,0:T(8,128)S(1)} %copy-done.6, f32[96,1024]{1,0:T(8,128)S(1)} %copy-done.4), kind=kOutput, calls=%fused_computation | convolution fusion | flops 1272184832 | bytes 15122432 | tf_op jit(solution)/shard_map/csr,ct->srt/dot_general | solution.py:93
  (54 shorter events, 7.0 us)
Async XLA Ops:
  0.0 59.9 %copy-start = (f32[16,7,64]{2,0,1:T(8,128)S(1)}, f32[16,7,64]{2,0,1:T(8,128)}, u32[]{:S(2)}) copy-start(f32[16,7,64]{2,0,1:T(8,128)} %param.3) | copy-start | bytes 86020
  1.6 0.7 copy-start.3
  1.6 0.9 copy-start.5
  52.8 141.3 %all-to-all-start.1 = ((bf16[8,2,6,640,80]{3,4,2,1,0:T(8,128)(2,1)}), bf16[8,2,6,640,80]{3,4,2,1,0:T(8,128)(2,1)}, u32[]{:S(2)}, u32[]{:S(2)}) async-start(bf16[8,2,6,640,80]{3,4,2,1,0:T(8,128)(2,1)} %stack.38), calls=%async_computation.1 | async-start | bytes 19660800 | tf_op jit(solution)/shard_map/all_to_all | solution.py:75
  209.9 3.9 %copy-start.2 = (bf16[1,6,640,8,80]{2,4,3,1,0:T(8,128)(2,1)S(1)}, bf16[1,6,640,8,80]{2,4,3,1,0:T(8,128)(2,1)}, u32[]{:S(2)}) copy-start(bf16[1,6,640,8,80]{2,4,3,1,0:T(8,128)(2,1)} %get-tuple-element.6) | copy-start | bytes 14745604
  234.9 30.7 %slice-start = ((s8[6553600]{0:T(1024)(128)(4,1)}), s8[4194304]{0:T(1024)(128)(4,1)S(1)}, s32[]{:S(2)}) async-start(s8[6553600]{0:T(1024)(128)(4,1)} %bitcast.129), calls=%async_computation.3 | async-start | bytes 8388608
  264.9 1.7 slice-start.1
  265.3 1.4 copy-start.4
  265.3 1.5 copy-start.6
  266.8 4.0 %copy-start.1 = (f32[16,7,64]{2,0,1:T(8,128)S(1)}, f32[16,7,64]{2,0,1:T(8,128)}, u32[]{:S(2)}) copy-start(f32[16,7,64]{2,0,1:T(8,128)} %param.3) | copy-start | bytes 86020
